TPU v7x, 512 devices: a whole 4x8x8 slice. The times are simulated.
512 devices in a mesh: chan: 128 (over z, y_hi, x), section: 4 (over y_lo, core).
Axes of the slice: x: 4, y: 8 (y_hi: 4, y_lo: 2; y = y_hi * 2 + y_lo), z: 8, core: 2. Of those that a mesh axis runs over, the one named last changes fastest.
Arguments:
- voltages: bfloat16 [2, 2, 36, 256, 188, 128], P(None, None, 'section', 'chan'), may hold values from -32 to 32
- weights: bfloat16 [2, 36, 256, 36, 188], P(None, 'section', 'chan'), may hold values from -4 to 4
- sat_index: int32 [2, 128, 2], P(None, 'chan'), may hold values from 0 to 63, as said below
- offsets: int32 [2, 128], replicated, may hold values from 0 to 127
- angles: float32 [64, 188], replicated, may hold values from -3 to 3
Outputs:
- visibilities: float32 [2, 36, 256, 1296], P(None, 'section', 'chan')
- new_weights: bfloat16 [2, 36, 256, 36, 188], P(None, 'section', 'chan')
Inputs may be any that keep to these rules, and one draw needn't show every extreme that they name: `sat_index`: catalogue rows of the satellites nulled in each cycle and block of 2 channels.
All inputs are finite; a program needn't handle non-finite values.
Results may differ from a plain program's by a relative error of at most 0.0065.
Values may be sent and summed in bfloat16 or wider, within the bound.
A program may use at most 128 MiB of HBM per device.

v0:
```python
import functools

import jax
import jax.numpy as jnp
from jax import lax
from jax.experimental import pallas as pl
from jax.experimental.pallas import tpu as pltpu
from jax.sharding import PartitionSpec as P

LOADING = 100.0
MESH = pl.DeviceIdType.MESH
F32 = jnp.float32
BF16 = jnp.bfloat16
CYC, DISH, CH, BEAM, PORT, TIME = 2, 9, 2, 36, 188, 128
SEC = 4
ROWS = CH * PORT
LANES = 384
TILES = LANES // TIME
WR = BEAM * CH
PER = WR // SEC
BLK = DISH * PER
BLKP = 168
ALL = SEC * DISH
ALLP = 40


def dot(a, b):
    return lax.dot_general(a, b, (((1,), (0,)), ((), ())), preferred_element_type=F32)


def dot_t(a, b):
    return lax.dot_general(a, b, (((1,), (1,)), ((), ())), preferred_element_type=F32)


def iota(shape, dim):
    return lax.broadcasted_iota(jnp.int32, shape, dim)


def even_lanes(shape):
    return (iota(shape, 1) & 1) == 0


def split(x):
    high = x.astype(BF16)
    return high, (x - high.astype(F32)).astype(BF16)


def strided(ref, rows):
    return jnp.concatenate([ref[k, rows, :] for k in range(TILES)], axis=1)


def lane_up(x):
    return pltpu.roll(x, 1, 1)


def lane_down(x):
    return pltpu.roll(x, LANES - 1, 1)


def kernel(
    chans,
    volt, w_in, sat_in, offs, table,
    vis, w_out,
    x, we, sat_l, sat_r, steer, vv, packed, halo_l, halo_r, ana, syn, nul, stage, sbuf, recv, wide, corr,
    x_sem, sat_ssem, sat_rsem, halo_ssem, halo_rsem, beam_ssem, beam_rsem,
):
    me = lax.axis_index("chan")
    sec = lax.axis_index("section")
    left = lax.rem(me + chans - 1, chans)
    right = lax.rem(me + 1, chans)

    def load(c, d, z):
        return pltpu.make_async_copy(
            volt.at[c, z, d],
            x.at[c, d, pl.ds(0, ROWS), pl.ds(z * TIME, TIME)],
            x_sem.at[c, d, z],
        )

    for c in range(CYC):
        for d in range(DISH):
            for z in range(2):
                load(c, d, z).start()

    barrier = pltpu.get_barrier_semaphore()
    for j in range(1, SEC):
        pl.semaphore_signal(
            barrier, inc=1, device_id={"section": lax.rem(sec + j, SEC)}, device_id_type=MESH
        )
    for peer in (left, right):
        pl.semaphore_signal(barrier, inc=1, device_id={"chan": peer}, device_id_type=MESH)
    pl.semaphore_wait(barrier, SEC + 1)

    def sat_copy(side):
        return pltpu.make_async_remote_copy(
            src_ref=sat_in,
            dst_ref=sat_r if side == 0 else sat_l,
            send_sem=sat_ssem.at[side],
            recv_sem=sat_rsem.at[side],
            device_id={"chan": left if side == 0 else right},
            device_id_type=MESH,
        )

    for side in range(2):
        sat_copy(side).start()

    spread = (lax.shift_right_logical(iota((PORT, LANES), 1), 1) == iota((PORT, LANES), 0)).astype(
        F32
    ).astype(BF16)
    own = (iota((WR, LANES), 0) & 1) == (iota((WR, LANES), 1) & 1)
    for c in range(CYC):
        for d in range(DISH):
            x[c, d, pl.ds(ROWS, LANES - ROWS), :] = jnp.zeros((LANES - ROWS, 2 * TIME), BF16)
    wide[:, pl.ds(ALL * PER, (ALLP - ALL) * PER), :] = jnp.zeros(
        (2 * CYC, (ALLP - ALL) * PER, TIME), F32
    )
    for d in range(DISH):
        for z in range(2):
            grown = dot(w_in[z, d], spread)
            we[d, pl.ds(z * WR, WR), :] = jnp.where(own, grown, 0.0).astype(BF16)

    def beams(c):
        for d in range(DISH):
            if c == 0:
                load(c, d, 0).wait()
                load(c, d, 1).wait()
            both = dot(we[d], x[c, d])
            real = both[:WR, :TIME] + both[WR:, TIME:]
            imag = both[:WR, TIME:] - both[WR:, :TIME]
            for s in range(SEC):
                rows = pl.ds(d * PER, PER)
                stage[s, rows, pl.ds(0, TIME)] = real[s * PER : (s + 1) * PER]
                stage[s, rows, pl.ds(TIME, TIME)] = imag[s * PER : (s + 1) * PER]
        for s in range(SEC):
            sbuf[c, s] = stage[s].astype(BF16)

    def beam_copy(c, j):
        peer = lax.rem(sec + j, SEC)
        return pltpu.make_async_remote_copy(
            src_ref=sbuf.at[c, peer],
            dst_ref=recv.at[c, sec],
            send_sem=beam_ssem.at[c, j - 1],
            recv_sem=beam_rsem.at[c, j - 1],
            device_id={"section": peer},
            device_id_type=MESH,
        )

    def send_beams(c):
        for j in (2, 3, 1):
            beam_copy(c, j).start()
        recv[c, sec] = sbuf[c, sec]

    beams(0)
    send_beams(0)

    grown_table = []
    for z in range(2):
        for part in split(table[z]):
            grown_table.append(dot(part, spread).astype(BF16))
    for side in range(2):
        sat_copy(side).wait()
    row = iota((8, TIME), 0)
    keep = (iota((8, LANES), 0) >= 4) == ((iota((8, LANES), 1) & 1) == 1)
    for c in range(CYC):
        index = jnp.where(
            (row & 3) < 2, sat_in[c], jnp.where(row < 4, sat_l[c], sat_r[c])
        )
        hot = (index == iota((8, TIME), 1)).astype(F32).astype(BF16)[:, :64]
        parts = [dot(hot, part) for part in grown_table]
        for i, (h, l) in enumerate(((0, 1), (2, 3))):
            steer[c, i] = parts[h] + parts[l]
        stacked = [jnp.where(keep, parts[i], 0.0) for i in (0, 2, 1, 3)]
        for i in range(4):
            ana[c, pl.ds(8 * i, 8), :] = stacked[i]

    even4 = even_lanes((4, LANES))

    def null_vectors(c):
        times = (offs[pl.ds(c, 1), :] == iota((TIME, TIME), 0)).astype(F32).astype(BF16)
        count = dot_t(jnp.ones((8, TIME), BF16), times)
        probe = ana[c].astype(BF16)
        for d in range(DISH):
            if c == 1:
                load(c, d, 0).wait()
                load(c, d, 1).wait()
            block = x[c, d]
            out = dot(probe, block)
            out = out[:16] + out[16:]
            y_real = (out[:8, :TIME] + out[8:, TIME:]) * count
            y_imag = (out[8:, :TIME] - out[:8, TIME:]) * count
            lines = jnp.concatenate(
                [
                    jnp.concatenate([y_real, -y_imag], axis=1),
                    jnp.concatenate([y_imag, y_real], axis=1),
                ],
                axis=0,
            )
            high, low = split(lines)
            back = dot_t(high, block) + dot_t(low, block)
            for i in range(2):
                kept = jnp.where(even4, back[8 * i : 8 * i + 4], back[8 * i + 4 : 8 * i + 8])
                for k in range(TILES):
                    vv[c, k, pl.ds(8 * d + 4 * i, 4), :] = kept[:, k * TIME : (k + 1) * TIME]

    even = even_lanes((DISH, LANES))

    def halo_copy(c, side):
        return pltpu.make_async_remote_copy(
            src_ref=packed.at[c, side],
            dst_ref=(halo_r if side == 0 else halo_l).at[c],
            send_sem=halo_ssem.at[c, side],
            recv_sem=halo_rsem.at[c, side],
            device_id={"chan": left if side == 0 else right},
            device_id_type=MESH,
        )

    def take(c, q):
        return strided(vv.at[c], pl.ds(q, DISH, stride=8))

    def send_halo(c):
        for i in range(2):
            first, second = take(c, 4 * i + 2), take(c, 4 * i + 3)
            packed[c, 0, i, pl.ds(0, DISH), :] = jnp.where(even, first, lane_up(second))
            packed[c, 1, i, pl.ds(0, DISH), :] = jnp.where(even, lane_down(first), second)
        for side in range(2):
            halo_copy(c, side).start()

    packed[...] = jnp.zeros_like(packed)
    null_vectors(0)
    send_halo(0)
    null_vectors(1)
    send_halo(1)

    def lane_sum(v):
        e = jnp.sum(jnp.where(even, v, 0.0), axis=1, keepdims=True)
        o = jnp.sum(jnp.where(even, 0.0, v), axis=1, keepdims=True)
        return jnp.where(even, e, o)

    def project_vectors(c):
        for side in range(2):
            halo_copy(c, side).wait()
        u = []
        for i in range(2):
            from_l = jnp.where(me == 0, 0.0, halo_l[c, i, pl.ds(0, DISH), :])
            from_r = jnp.where(me == chans - 1, 0.0, halo_r[c, i, pl.ds(0, DISH), :])
            halo = (
                jnp.where(even, from_l, lane_up(from_r)),
                jnp.where(even, lane_down(from_l), from_r),
            )
            for s in range(2):
                v = take(c, 4 * i + s)
                v = v + jnp.where(even, lane_down(v), lane_up(v))
                u.append(v + halo[s] + LOADING * steer[c, i, pl.ds(s, 1), :])
        u0r, u1r, u0i, u1i = u
        inv0 = 1.0 / lane_sum(u0r * u0r + u0i * u0i)
        inv1 = 1.0 / lane_sum(u1r * u1r + u1i * u1i)
        t0r, t0i = u0r * inv0, u0i * inv0
        kr = lane_sum(t0r * u1r + t0i * u1i)
        ki = lane_sum(t0r * u1i - t0i * u1r)
        t1r = (u1r - (u0r * kr - u0i * ki)) * inv1
        t1i = (u1i - (u0r * ki + u0i * kr)) * inv1
        for q, (t, v) in enumerate(((t0r, u0r), (t0i, u0i), (t1r, u1r), (t1i, u1i))):
            for k in range(TILES):
                syn[k, pl.ds(16 * q, DISH), :] = t[:, k * TIME : (k + 1) * TIME]
            nul[pl.ds(16 * q, DISH), :] = v

    def project(d):
        high, low = split(strided(syn, pl.ds(d, 4, stride=16)))
        old = we[d]
        g = dot_t(old, high) + dot_t(old, low)
        gr, gi = g[:WR], g[WR:]
        v = [nul[pl.ds(16 * q + d, 1), :] for q in range(4)]
        new_r = old[:WR].astype(F32)
        new_i = old[WR:].astype(F32)
        for s in range(2):
            cr = gr[:, 2 * s : 2 * s + 1] + gi[:, 2 * s + 1 : 2 * s + 2]
            ci = gi[:, 2 * s : 2 * s + 1] - gr[:, 2 * s + 1 : 2 * s + 2]
            vr, vi = v[2 * s], v[2 * s + 1]
            new_r = new_r - (vr * cr - vi * ci)
            new_i = new_i - (vr * ci + vi * cr)
        we[d, pl.ds(0, WR), :] = jnp.where(own, new_r, 0.0).astype(BF16)
        we[d, pl.ds(WR, WR), :] = jnp.where(own, new_i, 0.0).astype(BF16)

    project_vectors(0)
    for d in range(DISH):
        project(d)
    beams(1)
    send_beams(1)

    project_vectors(1)
    gather = (lax.shift_right_logical(iota((LANES, PORT), 0), 1) == iota((LANES, PORT), 1)).astype(
        F32
    ).astype(BF16)
    for d in range(DISH):
        project(d)
    for d in range(DISH):
        for z in range(2):
            w_out[z, d] = dot(we[d, pl.ds(z * WR, WR), :], gather).astype(BF16)

    for c in range(CYC):
        for j in range(1, SEC):
            beam_copy(c, j).wait_recv()
        for s in range(SEC):
            block = recv[c, s].astype(F32)[:BLK]
            for z in range(2):
                wide[2 * c + z, pl.ds(s * BLK, BLK), :] = block[:, z * TIME : (z + 1) * TIME]

    for r in range(PER):
        lanes = [wide[k, pl.ds(r, ALLP, stride=PER), :] for k in range(2 * CYC)]
        straight = jnp.concatenate(lanes, axis=1)
        turned = jnp.concatenate([lanes[1], -lanes[0], lanes[3], -lanes[2]], axis=1)
        right_side = straight.astype(BF16)
        result = dot_t(jnp.concatenate([straight, turned], axis=0).astype(BF16), right_side)
        result = result * (1.0 / (CYC * TIME))
        for z in range(2):
            corr[z, pl.ds(r * ALLP, ALLP), pl.ds(0, ALLP)] = result[z * ALLP : (z + 1) * ALLP]
    for z in range(2):
        for d in range(ALL):
            vis[z, :, pl.ds(d * ALL, ALL)] = corr[z, pl.ds(d, PER, stride=ALLP), :][:, :ALL]

    for c in range(CYC):
        for j in range(1, SEC):
            beam_copy(c, j).wait_send()


def per_device(chans, voltages, weights, sat_index, offsets, angles):
    volt = voltages.transpose(0, 1, 2, 4, 3, 5).reshape(CYC, 2, DISH, ROWS, TIME)
    w_in = weights.transpose(0, 1, 3, 2, 4).reshape(2, DISH, WR, PORT)
    sat = jnp.broadcast_to(sat_index.reshape(CYC, 1, 2, 1), (CYC, 4, 2, TIME)).reshape(CYC, 8, TIME)
    table = jnp.stack([jnp.cos(angles), jnp.sin(angles)])
    vmem = pl.BlockSpec(memory_space=pltpu.VMEM)
    dma = pltpu.SemaphoreType.DMA
    vis, new = pl.pallas_call(
        functools.partial(kernel, chans),
        out_shape=(
            jax.ShapeDtypeStruct((2, PER, ALL * ALL), F32),
            jax.ShapeDtypeStruct((2, DISH, WR, PORT), BF16),
        ),
        in_specs=[pl.BlockSpec(memory_space=pl.ANY), vmem, vmem, vmem, vmem],
        out_specs=(vmem, vmem),
        scratch_shapes=[
            pltpu.VMEM((CYC, DISH, LANES, 2 * TIME), BF16),
            pltpu.VMEM((DISH, 2 * WR, LANES), BF16),
            pltpu.VMEM((CYC, 8, TIME), jnp.int32),
            pltpu.VMEM((CYC, 8, TIME), jnp.int32),
            pltpu.VMEM((CYC, 2, 8, LANES), F32),
            pltpu.VMEM((CYC, TILES, DISH * 8, TIME), F32),
            pltpu.VMEM((CYC, 2, 2, 16, LANES), F32),
            pltpu.VMEM((CYC, 2, 16, LANES), F32),
            pltpu.VMEM((CYC, 2, 16, LANES), F32),
            pltpu.VMEM((CYC, 32, LANES), F32),
            pltpu.VMEM((TILES, 64, TIME), F32),
            pltpu.VMEM((64, LANES), F32),
            pltpu.VMEM((SEC, BLKP, 2 * TIME), F32),
            pltpu.VMEM((CYC, SEC, BLKP, 2 * TIME), BF16),
            pltpu.VMEM((CYC, SEC, BLKP, 2 * TIME), BF16),
            pltpu.VMEM((2 * CYC, ALLP * PER, TIME), F32),
            pltpu.VMEM((2, PER * ALLP, TIME), F32),
            dma((CYC, DISH, 2)),
            dma((2,)),
            dma((2,)),
            dma((CYC, 2)),
            dma((CYC, 2)),
            dma((CYC, SEC - 1)),
            dma((CYC, SEC - 1)),
        ],
        compiler_params=pltpu.CompilerParams(collective_id=0, has_side_effects=True),
    )(volt, w_in, sat, offsets, table)
    visibility = vis.reshape(2, DISH, CH, ALL * ALL)
    new = new.reshape(2, DISH, BEAM, CH, PORT).transpose(0, 1, 3, 2, 4)
    return visibility, new


def solution(mesh):
    placed = (
        P(None, None, "section", "chan", None, None),
        P(None, "section", "chan", None, None),
        P(None, "chan", None),
        P(),
        P(),
    )
    return jax.shard_map(
        functools.partial(per_device, mesh.shape["chan"]),
        mesh=mesh,
        in_specs=placed,
        out_specs=(P(None, "section", "chan", None), P(None, "section", "chan", None, None)),
        check_vma=False,
    )
```

profile of v0, /device:TPU:1, one launch (start us, length us, event | category | flops | bytes accessed | tf_op | source)
XLA Modules:
  0.0 51.5 jit_solution(6165870275756064687)
XLA Ops:
  0.6 0.7 %broadcast_in_dim.12 = s32[2,4,2]{2,1,0:T(4,128)S(1)} broadcast(s32[2,2]{1,0:T(2,128)} %bitcast.17), dimensions={0,2} | broadcast | bytes 80 | tf_op jit(solution)/shard_map/broadcast_in_dim | solution.py:328
  1.3 0.1 broadcast_in_dim.13
  1.4 0.7 %broadcast_in_dim.14.sat_in = s32[2,8,128]{2,1,0:T(8,128)} broadcast(s32[2,8]{1,0:T(2,128)S(1)} %broadcast_in_dim.13), dimensions={0,1} | broadcast | bytes 8256 | tf_op jit(solution)/shard_map/broadcast_in_dim | solution.py:328
  2.1 1.1 %cosine_bitcast_fusion = (f32[1,64,188]{2,1,0:T(8,128)S(1)}, f32[1,64,188]{2,1,0:T(8,128)S(1)}) fusion(f32[64,188]{1,0:T(8,128)} %param.9), kind=kLoop, calls=%fused_computation.2 | loop fusion | bytes 144384 | tf_op jit(solution)/shard_map/stack | solution.py:329
  3.1 0.7 %pad_maximum_fusion.table = f32[2,64,188]{2,1,0:T(8,128)} fusion(f32[1,64,188]{2,1,0:T(8,128)S(1)} %get-tuple-element.9, f32[1,64,188]{2,1,0:T(8,128)S(1)} %get-tuple-element.8), kind=kLoop, calls=%fused_computation | loop fusion | flops 24064 | bytes 192512 | tf_op jit(solution)/shard_map/stack | solution.py:329
  3.8 2.7 %reshape.21.w_in = bf16[2,9,72,188]{3,2,1,0:T(8,128)(2,1)} reshape(bf16[2,9,36,2,188]{4,3,2,1,0:T(2,128)(2,1)} %bitcast.15) | data formatting | bytes 974592 | tf_op jit(solution)/shard_map/reshape | solution.py:327
  6.5 40.5 %shard_map.68 = (f32[2,18,1296]{2,1,0:T(8,128)}, bf16[2,9,72,188]{3,2,1,0:T(8,128)(2,1)}) custom-call(bf16[2,2,9,376,128]{4,3,2,1,0:T(8,128)(2,1)} %bitcast.13, bf16[2,9,72,188]{3,2,1,0:T(8,128)(2,1)} %reshape.21.w_in, s32[2,8,128]{2,1,0:T(8,128)} %broadcast_in_dim.14.sat_in, s32[2,128]{1,0:T(2,128)} %offs.1, f32[2,64,188]{2,1,0:T(8,128)} %pad_maximum_fusion.table), custom_call_target="tpu_custom_call" | custom-call | tf_op jit(solution)/shard_map/pallas_call | solution.py:332
  47.0 1.1 %copy.7 = f32[2,18,1296]{2,0,1:T(2,128)S(1)} copy(f32[2,18,1296]{2,1,0:T(8,128)} %get-tuple-element.4) | data formatting | bytes 373248 | tf_op jit(solution)/shard_map/pallas_call | solution.py:332
  48.1 0.8 %copy.8 = f32[2,9,2,1296]{3,2,1,0:T(2,128)} copy(f32[2,9,2,1296]{3,0,2,1:T(2,128)S(1)} %bitcast.14) | data formatting | bytes 373248
  48.9 2.6 %reshape.23 = bf16[2,9,36,2,188]{4,3,2,1,0:T(2,128)(2,1)} reshape(bf16[2,9,72,188]{3,2,1,0:T(8,128)(2,1)} %get-tuple-element.5) | data formatting | bytes 974592 | tf_op jit(solution)/shard_map/reshape | solution.py:369
where the time goes:
time: 51.8 us; the launch traced here: 51.5 us
  Pallas kernels  40.5 us (78%)
  local copies, waits for them, and re-layouts  9.73 us (19%)
  other arithmetic  0.67 us (1%)
  between operations  0.65 us (1%)
    pallas_call x1, Pallas kernels, per_device(): pl.pallas_call(functools.partial(kernel, chans), out_shape=(jax.ShapeDtyp...  40.5 us
    reshape x1, local copies, waits for them, and re-layouts, per_device(): w_in = weights.transpose(0, 1, 3, 2, 4).reshape(2, DISH, WR, PORT)  2.73 us
    reshape x1, local copies, waits for them, and re-layouts, per_device(): new = new.reshape(2, DISH, BEAM, CH, PORT).transpose(0, 1, 3, 2, 4)  2.65 us
    broadcast_in_dim x3, local copies, waits for them, and re-layouts, per_device(): jnp.broadcast_to(sat_index.reshape(CYC, 1, 2, 1), (CYC, 4, 2, TIME))  1.43 us
    another operation x1, local copies, waits for them, and re-layouts, per_device(): table = jnp.stack([jnp.cos(angles), jnp.sin(angles)])  1.08 us
    pallas_call x1, local copies, waits for them, and re-layouts, per_device(): pl.pallas_call(functools.partial(kernel, chans), out_shape=(jax.ShapeDtyp...  1.06 us

commit v1 on v0

--- a/solution.py
+++ b/solution.py
@@ -59,10 +59,10 @@
 
 def kernel(
     chans,
-    volt, w_in, sat_in, offs, table,
+    volt, w_hbm, sat_hbm, offs_hbm, ang_hbm,
     vis, w_out,
-    x, we, sat_l, sat_r, steer, vv, packed, halo_l, halo_r, ana, syn, nul, stage, sbuf, recv, wide, corr,
-    x_sem, sat_ssem, sat_rsem, halo_ssem, halo_rsem, beam_ssem, beam_rsem,
+    x, w_in, sat_in, offs, ang, flat, we, sat_l, sat_r, steer, vv, packed, halo_l, halo_r, ana, syn, nul, stage, sbuf, recv, wide, corr,
+    in_sem, x_sem, sat_ssem, sat_rsem, halo_ssem, halo_rsem, beam_ssem, beam_rsem,
 ):
     me = lax.axis_index("chan")
     sec = lax.axis_index("section")
@@ -76,19 +76,35 @@
             x_sem.at[c, d, z],
         )
 
+    sat_l[...] = jnp.zeros_like(sat_l)
+    sat_r[...] = jnp.zeros_like(sat_r)
+    halo_l[...] = jnp.zeros_like(halo_l)
+    halo_r[...] = jnp.zeros_like(halo_r)
+
+    barrier = pltpu.get_barrier_semaphore()
+    for j in range(1, SEC):
+        pl.semaphore_signal(
+            barrier, inc=1, device_id={"section": lax.rem(sec + j, SEC)}, device_id_type=MESH
+        )
+    sides = ((me > 0, left), (me < chans - 1, right))
+    for exists, peer in sides:
+
+        @pl.when(exists)
+        def _():
+            pl.semaphore_signal(barrier, inc=1, device_id={"chan": peer}, device_id_type=MESH)
+
+    small = [
+        pltpu.make_async_copy(source, target, in_sem.at[i])
+        for i, (source, target) in enumerate(
+            ((ang_hbm, ang), (w_hbm, w_in), (sat_hbm, sat_in), (offs_hbm, offs))
+        )
+    ]
+    for copy in small:
+        copy.start()
     for c in range(CYC):
         for d in range(DISH):
             for z in range(2):
                 load(c, d, z).start()
-
-    barrier = pltpu.get_barrier_semaphore()
-    for j in range(1, SEC):
-        pl.semaphore_signal(
-            barrier, inc=1, device_id={"section": lax.rem(sec + j, SEC)}, device_id_type=MESH
-        )
-    for peer in (left, right):
-        pl.semaphore_signal(barrier, inc=1, device_id={"chan": peer}, device_id_type=MESH)
-    pl.semaphore_wait(barrier, SEC + 1)
 
     def sat_copy(side):
         return pltpu.make_async_remote_copy(
@@ -99,9 +115,6 @@
             device_id={"chan": left if side == 0 else right},
             device_id_type=MESH,
         )
-
-    for side in range(2):
-        sat_copy(side).start()
 
     spread = (lax.shift_right_logical(iota((PORT, LANES), 1), 1) == iota((PORT, LANES), 0)).astype(
         F32
@@ -113,10 +126,25 @@
     wide[:, pl.ds(ALL * PER, (ALLP - ALL) * PER), :] = jnp.zeros(
         (2 * CYC, (ALLP - ALL) * PER, TIME), F32
     )
+    small[0].wait()
+    grown_table = []
+    for values in (jnp.cos(ang[...]), jnp.sin(ang[...])):
+        for part in split(values):
+            grown_table.append(dot(part, spread).astype(BF16))
+    small[1].wait()
     for d in range(DISH):
         for z in range(2):
-            grown = dot(w_in[z, d], spread)
+            grown = dot(w_in[z, d].reshape(WR, PORT), spread)
             we[d, pl.ds(z * WR, WR), :] = jnp.where(own, grown, 0.0).astype(BF16)
+
+    pl.semaphore_wait(barrier, SEC - 1 + sum(e.astype(jnp.int32) for e, _peer in sides))
+    small[2].wait()
+    small[3].wait()
+    for side in range(2):
+
+        @pl.when(sides[side][0])
+        def _():
+            sat_copy(side).start()
 
     def beams(c):
         for d in range(DISH):
@@ -152,18 +180,20 @@
     beams(0)
     send_beams(0)
 
-    grown_table = []
-    for z in range(2):
-        for part in split(table[z]):
-            grown_table.append(dot(part, spread).astype(BF16))
     for side in range(2):
-        sat_copy(side).wait()
+
+        @pl.when(sides[1 - side][0])
+        def _():
+            sat_copy(side).wait_recv()
+
     row = iota((8, TIME), 0)
     keep = (iota((8, LANES), 0) >= 4) == ((iota((8, LANES), 1) & 1) == 1)
     for c in range(CYC):
-        index = jnp.where(
-            (row & 3) < 2, sat_in[c], jnp.where(row < 4, sat_l[c], sat_r[c])
-        )
+        own_s, left_s, right_s = (
+            jnp.where((row & 1) == 0, ref[pl.ds(c, 1), pl.ds(0, 1)], ref[pl.ds(c, 1), pl.ds(1, 1)])
+            for ref in (sat_in, sat_l, sat_r)
+        )
+        index = jnp.where((row & 3) < 2, own_s, jnp.where(row < 4, left_s, right_s))
         hot = (index == iota((8, TIME), 1)).astype(F32).astype(BF16)[:, :64]
         parts = [dot(hot, part) for part in grown_table]
         for i, (h, l) in enumerate(((0, 1), (2, 3))):
@@ -222,7 +252,10 @@
             packed[c, 0, i, pl.ds(0, DISH), :] = jnp.where(even, first, lane_up(second))
             packed[c, 1, i, pl.ds(0, DISH), :] = jnp.where(even, lane_down(first), second)
         for side in range(2):
-            halo_copy(c, side).start()
+
+            @pl.when(sides[side][0])
+            def _():
+                halo_copy(c, side).start()
 
     packed[...] = jnp.zeros_like(packed)
     null_vectors(0)
@@ -237,11 +270,15 @@
 
     def project_vectors(c):
         for side in range(2):
-            halo_copy(c, side).wait()
+
+            @pl.when(sides[1 - side][0])
+            def _():
+                halo_copy(c, side).wait_recv()
+
         u = []
         for i in range(2):
-            from_l = jnp.where(me == 0, 0.0, halo_l[c, i, pl.ds(0, DISH), :])
-            from_r = jnp.where(me == chans - 1, 0.0, halo_r[c, i, pl.ds(0, DISH), :])
+            from_l = halo_l[c, i, pl.ds(0, DISH), :]
+            from_r = halo_r[c, i, pl.ds(0, DISH), :]
             halo = (
                 jnp.where(even, from_l, lane_up(from_r)),
                 jnp.where(even, lane_down(from_l), from_r),
@@ -294,7 +331,8 @@
         project(d)
     for d in range(DISH):
         for z in range(2):
-            w_out[z, d] = dot(we[d, pl.ds(z * WR, WR), :], gather).astype(BF16)
+            dense = dot(we[d, pl.ds(z * WR, WR), :], gather).astype(BF16)
+            w_out[z, d] = dense.reshape(BEAM, CH, PORT)
 
     for c in range(CYC):
         for j in range(1, SEC):
@@ -315,33 +353,46 @@
             corr[z, pl.ds(r * ALLP, ALLP), pl.ds(0, ALLP)] = result[z * ALLP : (z + 1) * ALLP]
     for z in range(2):
         for d in range(ALL):
-            vis[z, :, pl.ds(d * ALL, ALL)] = corr[z, pl.ds(d, PER, stride=ALLP), :][:, :ALL]
+            flat[z, :, pl.ds(d * ALL, ALL)] = corr[z, pl.ds(d, PER, stride=ALLP), :][:, :ALL]
+        vis[z] = flat[z].reshape(DISH, CH, ALL * ALL)
 
     for c in range(CYC):
         for j in range(1, SEC):
             beam_copy(c, j).wait_send()
+    for side in range(2):
+
+        @pl.when(sides[side][0])
+        def _():
+            sat_copy(side).wait_send()
+            for c in range(CYC):
+                halo_copy(c, side).wait_send()
 
 
 def per_device(chans, voltages, weights, sat_index, offsets, angles):
     volt = voltages.transpose(0, 1, 2, 4, 3, 5).reshape(CYC, 2, DISH, ROWS, TIME)
-    w_in = weights.transpose(0, 1, 3, 2, 4).reshape(2, DISH, WR, PORT)
-    sat = jnp.broadcast_to(sat_index.reshape(CYC, 1, 2, 1), (CYC, 4, 2, TIME)).reshape(CYC, 8, TIME)
-    table = jnp.stack([jnp.cos(angles), jnp.sin(angles)])
+    w_in = weights.transpose(0, 1, 3, 2, 4)
+    sat = sat_index.reshape(CYC, 2)
     vmem = pl.BlockSpec(memory_space=pltpu.VMEM)
+    hbm = pl.BlockSpec(memory_space=pltpu.HBM)
     dma = pltpu.SemaphoreType.DMA
     vis, new = pl.pallas_call(
         functools.partial(kernel, chans),
         out_shape=(
-            jax.ShapeDtypeStruct((2, PER, ALL * ALL), F32),
-            jax.ShapeDtypeStruct((2, DISH, WR, PORT), BF16),
+            jax.ShapeDtypeStruct((2, DISH, CH, ALL * ALL), F32),
+            jax.ShapeDtypeStruct((2, DISH, BEAM, CH, PORT), BF16),
         ),
-        in_specs=[pl.BlockSpec(memory_space=pl.ANY), vmem, vmem, vmem, vmem],
+        in_specs=[hbm] * 5,
         out_specs=(vmem, vmem),
         scratch_shapes=[
             pltpu.VMEM((CYC, DISH, LANES, 2 * TIME), BF16),
+            pltpu.VMEM((2, DISH, BEAM, CH, PORT), BF16),
+            pltpu.VMEM((CYC, 2), jnp.int32),
+            pltpu.VMEM((CYC, TIME), jnp.int32),
+            pltpu.VMEM((64, PORT), F32),
+            pltpu.VMEM((2, PER, ALL * ALL), F32),
             pltpu.VMEM((DISH, 2 * WR, LANES), BF16),
-            pltpu.VMEM((CYC, 8, TIME), jnp.int32),
-            pltpu.VMEM((CYC, 8, TIME), jnp.int32),
+            pltpu.VMEM((CYC, 2), jnp.int32),
+            pltpu.VMEM((CYC, 2), jnp.int32),
             pltpu.VMEM((CYC, 2, 8, LANES), F32),
             pltpu.VMEM((CYC, TILES, DISH * 8, TIME), F32),
             pltpu.VMEM((CYC, 2, 2, 16, LANES), F32),
@@ -355,6 +406,7 @@
             pltpu.VMEM((CYC, SEC, BLKP, 2 * TIME), BF16),
             pltpu.VMEM((2 * CYC, ALLP * PER, TIME), F32),
             pltpu.VMEM((2, PER * ALLP, TIME), F32),
+            dma((4,)),
             dma((CYC, DISH, 2)),
             dma((2,)),
             dma((2,)),
@@ -363,11 +415,11 @@
             dma((CYC, SEC - 1)),
             dma((CYC, SEC - 1)),
         ],
-        compiler_params=pltpu.CompilerParams(collective_id=0, has_side_effects=True),
-    )(volt, w_in, sat, offsets, table)
-    visibility = vis.reshape(2, DISH, CH, ALL * ALL)
-    new = new.reshape(2, DISH, BEAM, CH, PORT).transpose(0, 1, 3, 2, 4)
-    return visibility, new
+        compiler_params=pltpu.CompilerParams(
+            collective_id=0, has_side_effects=True, vmem_limit_bytes=24 << 20
+        ),
+    )(*(pltpu.with_memory_space_constraint(a, pltpu.HBM) for a in (volt, w_in, sat, offsets, angles)))
+    return vis, new.transpose(0, 1, 3, 2, 4)
 
 
 def solution(mesh):

time: 51.8 us -> 30.6 us (0.59)
  the two profiles are of different devices: /device:TPU:1 before, /device:TPU:257 now
where the time goes in v1:
time: 30.6 us; the launch traced here: 30.5 us
  Pallas kernels  28.3 us (92%)
  local copies, waits for them, and re-layouts  1.52 us (5%)
  between operations  0.64 us (2%)
    pallas_call x1, Pallas kernels, per_device(): pl.pallas_call(functools.partial(kernel, chans), out_shape=(jax.ShapeDtyp...  28.3 us
    unnamed x2, local copies, waits for them, and re-layouts  1.52 us

profile of v1, /device:TPU:257, one launch (start us, length us, event | category | flops | bytes accessed | tf_op | source)
XLA Modules:
  0.0 30.5 jit_solution(16437311495003553574)
XLA Ops:
  0.6 28.3 %shard_map.68 = (f32[2,9,2,1296]{3,2,1,0:T(2,128)S(1)}, bf16[2,9,36,2,188]{4,3,2,1,0:T(2,128)(2,1)S(1)}) custom-call(bf16[2,2,9,376,128]{4,3,2,1,0:T(8,128)(2,1)} %bitcast.7, bf16[2,9,36,2,188]{4,3,2,1,0:T(2,128)(2,1)} %bitcast.8, s32[2,2]{1,0:T(2,128)} %bitcast.9, s32[2,128]{1,0:T(2,128)} %offs_hbm.1, f32[64,188]{1,0:T(8,128)} %ang_hbm.1), custom_call_target="tpu_custom_call" | custom-call | tf_op jit(solution)/shard_map/pallas_call | solution.py:378
  29.0 0.7 %copy.9 = f32[2,9,2,1296]{3,2,1,0:T(2,128)} copy(f32[2,9,2,1296]{3,2,1,0:T(2,128)S(1)} %get-tuple-element.8) | data formatting | bytes 373248
  29.7 0.8 %copy.10 = bf16[2,9,2,36,188]{4,2,3,1,0:T(2,128)(2,1)} copy(bf16[2,9,2,36,188]{4,2,3,1,0:T(2,128)(2,1)S(1)} %bitcast.6) | data formatting | bytes 974592

commit v2 on v1

--- a/solution.py
+++ b/solution.py
@@ -18,8 +18,10 @@
 TILES = LANES // TIME
 WR = BEAM * CH
 PER = WR // SEC
-BLK = DISH * PER
-BLKP = 168
+PARTS = 3
+PART = DISH // PARTS
+BLK = PART * PER
+BLKP = 56
 ALL = SEC * DISH
 ALLP = 40
 
@@ -60,8 +62,8 @@
 def kernel(
     chans,
     volt, w_hbm, sat_hbm, offs_hbm, ang_hbm,
-    vis, w_out,
-    x, w_in, sat_in, offs, ang, flat, we, sat_l, sat_r, steer, vv, packed, halo_l, halo_r, ana, syn, nul, stage, sbuf, recv, wide, corr,
+    wide, w_out,
+    x, w_in, sat_in, offs, ang, we, sat_l, sat_r, steer, vv, pack, packed, halo_l, halo_r, ana, syn, nul, stage, sbuf, recv,
     in_sem, x_sem, sat_ssem, sat_rsem, halo_ssem, halo_rsem, beam_ssem, beam_rsem,
 ):
     me = lax.axis_index("chan")
@@ -115,6 +117,14 @@
             device_id={"chan": left if side == 0 else right},
             device_id_type=MESH,
         )
+
+    pl.semaphore_wait(barrier, SEC - 1 + sum(e.astype(jnp.int32) for e, _peer in sides))
+    small[2].wait()
+    for side in range(2):
+
+        @pl.when(sides[side][0])
+        def _():
+            sat_copy(side).start()
 
     spread = (lax.shift_right_logical(iota((PORT, LANES), 1), 1) == iota((PORT, LANES), 0)).astype(
         F32
@@ -137,17 +147,11 @@
             grown = dot(w_in[z, d].reshape(WR, PORT), spread)
             we[d, pl.ds(z * WR, WR), :] = jnp.where(own, grown, 0.0).astype(BF16)
 
-    pl.semaphore_wait(barrier, SEC - 1 + sum(e.astype(jnp.int32) for e, _peer in sides))
-    small[2].wait()
-    small[3].wait()
-    for side in range(2):
-
-        @pl.when(sides[side][0])
-        def _():
-            sat_copy(side).start()
-
-    def beams(c):
-        for d in range(DISH):
+    def beams(c, k):
+        dishes = range(PART * k, PART * (k + 1))
+        if c == 1:
+            project(dishes)
+        for j, d in enumerate(dishes):
             if c == 0:
                 load(c, d, 0).wait()
                 load(c, d, 1).wait()
@@ -155,30 +159,31 @@
             real = both[:WR, :TIME] + both[WR:, TIME:]
             imag = both[:WR, TIME:] - both[WR:, :TIME]
             for s in range(SEC):
-                rows = pl.ds(d * PER, PER)
-                stage[s, rows, pl.ds(0, TIME)] = real[s * PER : (s + 1) * PER]
-                stage[s, rows, pl.ds(TIME, TIME)] = imag[s * PER : (s + 1) * PER]
+                rows = pl.ds(j * PER, PER)
+                stage[s, k, rows, pl.ds(0, TIME)] = real[s * PER : (s + 1) * PER]
+                stage[s, k, rows, pl.ds(TIME, TIME)] = imag[s * PER : (s + 1) * PER]
         for s in range(SEC):
-            sbuf[c, s] = stage[s].astype(BF16)
-
-    def beam_copy(c, j):
+            sbuf[c, s, k] = stage[s, k].astype(BF16)
+
+    def beam_copy(c, k, j):
         peer = lax.rem(sec + j, SEC)
         return pltpu.make_async_remote_copy(
-            src_ref=sbuf.at[c, peer],
-            dst_ref=recv.at[c, sec],
-            send_sem=beam_ssem.at[c, j - 1],
-            recv_sem=beam_rsem.at[c, j - 1],
+            src_ref=sbuf.at[c, peer, k],
+            dst_ref=recv.at[c, sec, k],
+            send_sem=beam_ssem.at[c, k, j - 1],
+            recv_sem=beam_rsem.at[c, k, j - 1],
             device_id={"section": peer},
             device_id_type=MESH,
         )
 
-    def send_beams(c):
+    def send_beams(c, k):
         for j in (2, 3, 1):
-            beam_copy(c, j).start()
-        recv[c, sec] = sbuf[c, sec]
-
-    beams(0)
-    send_beams(0)
+            beam_copy(c, k, j).start()
+        recv[c, sec, k] = sbuf[c, sec, k]
+
+    for k in range(PARTS):
+        beams(0, k)
+        send_beams(0, k)
 
     for side in range(2):
 
@@ -205,6 +210,8 @@
     even4 = even_lanes((4, LANES))
 
     def null_vectors(c):
+        if c == 0:
+            small[3].wait()
         times = (offs[pl.ds(c, 1), :] == iota((TIME, TIME), 0)).astype(F32).astype(BF16)
         count = dot_t(jnp.ones((8, TIME), BF16), times)
         probe = ana[c].astype(BF16)
@@ -225,7 +232,8 @@
                 axis=0,
             )
             high, low = split(lines)
-            back = dot_t(high, block) + dot_t(low, block)
+            back = dot_t(jnp.concatenate([high, low], axis=0), block)
+            back = back[:16] + back[16:]
             for i in range(2):
                 kept = jnp.where(even4, back[8 * i : 8 * i + 4], back[8 * i + 4 : 8 * i + 8])
                 for k in range(TILES):
@@ -249,15 +257,17 @@
     def send_halo(c):
         for i in range(2):
             first, second = take(c, 4 * i + 2), take(c, 4 * i + 3)
-            packed[c, 0, i, pl.ds(0, DISH), :] = jnp.where(even, first, lane_up(second))
-            packed[c, 1, i, pl.ds(0, DISH), :] = jnp.where(even, lane_down(first), second)
+            rows = pl.ds(i * DISH, DISH)
+            pack[0, rows, :] = jnp.where(even, first, lane_up(second))
+            pack[1, rows, :] = jnp.where(even, lane_down(first), second)
+        packed[c] = pack[...]
         for side in range(2):
 
             @pl.when(sides[side][0])
             def _():
                 halo_copy(c, side).start()
 
-    packed[...] = jnp.zeros_like(packed)
+    pack[...] = jnp.zeros_like(pack)
     null_vectors(0)
     send_halo(0)
     null_vectors(1)
@@ -276,9 +286,9 @@
                 halo_copy(c, side).wait_recv()
 
         u = []
+        halos = [ref[c] for ref in (halo_l, halo_r)]
         for i in range(2):
-            from_l = halo_l[c, i, pl.ds(0, DISH), :]
-            from_r = halo_r[c, i, pl.ds(0, DISH), :]
+            from_l, from_r = (h[i * DISH : (i + 1) * DISH] for h in halos)
             halo = (
                 jnp.where(even, from_l, lane_up(from_r)),
                 jnp.where(even, lane_down(from_l), from_r),
@@ -300,48 +310,68 @@
                 syn[k, pl.ds(16 * q, DISH), :] = t[:, k * TIME : (k + 1) * TIME]
             nul[pl.ds(16 * q, DISH), :] = v
 
-    def project(d):
-        high, low = split(strided(syn, pl.ds(d, 4, stride=16)))
-        old = we[d]
-        g = dot_t(old, high) + dot_t(old, low)
-        gr, gi = g[:WR], g[WR:]
-        v = [nul[pl.ds(16 * q + d, 1), :] for q in range(4)]
-        new_r = old[:WR].astype(F32)
-        new_i = old[WR:].astype(F32)
-        for s in range(2):
-            cr = gr[:, 2 * s : 2 * s + 1] + gi[:, 2 * s + 1 : 2 * s + 2]
-            ci = gi[:, 2 * s : 2 * s + 1] - gr[:, 2 * s + 1 : 2 * s + 2]
-            vr, vi = v[2 * s], v[2 * s + 1]
-            new_r = new_r - (vr * cr - vi * ci)
-            new_i = new_i - (vr * ci + vi * cr)
-        we[d, pl.ds(0, WR), :] = jnp.where(own, new_r, 0.0).astype(BF16)
-        we[d, pl.ds(WR, WR), :] = jnp.where(own, new_i, 0.0).astype(BF16)
+    def project(dishes):
+        inner = []
+        for d in dishes:
+            high, low = split(strided(syn, pl.ds(d, 4, stride=16)))
+            old = we[d]
+            inner.append(dot_t(old, high) + dot_t(old, low))
+        for d, g in zip(dishes, inner):
+            gr, gi = g[:WR], g[WR:]
+            v = [nul[pl.ds(16 * q + d, 1), :] for q in range(4)]
+            new_r = we[d, pl.ds(0, WR), :].astype(F32)
+            new_i = we[d, pl.ds(WR, WR), :].astype(F32)
+            for s in range(2):
+                cr = gr[:, 2 * s : 2 * s + 1] + gi[:, 2 * s + 1 : 2 * s + 2]
+                ci = gi[:, 2 * s : 2 * s + 1] - gr[:, 2 * s + 1 : 2 * s + 2]
+                vr, vi = v[2 * s], v[2 * s + 1]
+                new_r = new_r - (vr * cr - vi * ci)
+                new_i = new_i - (vr * ci + vi * cr)
+            we[d, pl.ds(0, WR), :] = jnp.where(own, new_r, 0.0).astype(BF16)
+            we[d, pl.ds(WR, WR), :] = jnp.where(own, new_i, 0.0).astype(BF16)
 
     project_vectors(0)
-    for d in range(DISH):
-        project(d)
-    beams(1)
-    send_beams(1)
+    for k in range(PARTS):
+        beams(1, k)
+        send_beams(1, k)
 
     project_vectors(1)
     gather = (lax.shift_right_logical(iota((LANES, PORT), 0), 1) == iota((LANES, PORT), 1)).astype(
         F32
     ).astype(BF16)
-    for d in range(DISH):
-        project(d)
+    for k in range(PARTS):
+        project(range(PART * k, PART * (k + 1)))
     for d in range(DISH):
         for z in range(2):
             dense = dot(we[d, pl.ds(z * WR, WR), :], gather).astype(BF16)
             w_out[z, d] = dense.reshape(BEAM, CH, PORT)
 
     for c in range(CYC):
-        for j in range(1, SEC):
-            beam_copy(c, j).wait_recv()
-        for s in range(SEC):
-            block = recv[c, s].astype(F32)[:BLK]
-            for z in range(2):
-                wide[2 * c + z, pl.ds(s * BLK, BLK), :] = block[:, z * TIME : (z + 1) * TIME]
-
+        for k in range(PARTS):
+            for j in range(1, SEC):
+                beam_copy(c, k, j).wait_recv()
+            for s in range(SEC):
+                block = recv[c, s, k].astype(F32)[:BLK]
+                rows = pl.ds((s * PARTS + k) * BLK, BLK)
+                for z in range(2):
+                    wide[2 * c + z, rows, :] = block[:, z * TIME : (z + 1) * TIME]
+
+    for c in range(CYC):
+        for k in range(PARTS):
+            for j in range(1, SEC):
+                beam_copy(c, k, j).wait_send()
+    for side in range(2):
+
+        @pl.when(sides[side][0])
+        def _():
+            sat_copy(side).wait_send()
+            for c in range(CYC):
+                halo_copy(c, side).wait_send()
+
+
+def correlate(wide, w_new, vis_hbm, w_hbm, vis, flat, corr, sems):
+    weights = pltpu.make_async_copy(w_new, w_hbm, sems.at[0])
+    weights.start()
     for r in range(PER):
         lanes = [wide[k, pl.ds(r, ALLP, stride=PER), :] for k in range(2 * CYC)]
         straight = jnp.concatenate(lanes, axis=1)
@@ -355,17 +385,10 @@
         for d in range(ALL):
             flat[z, :, pl.ds(d * ALL, ALL)] = corr[z, pl.ds(d, PER, stride=ALLP), :][:, :ALL]
         vis[z] = flat[z].reshape(DISH, CH, ALL * ALL)
-
-    for c in range(CYC):
-        for j in range(1, SEC):
-            beam_copy(c, j).wait_send()
-    for side in range(2):
-
-        @pl.when(sides[side][0])
-        def _():
-            sat_copy(side).wait_send()
-            for c in range(CYC):
-                halo_copy(c, side).wait_send()
+        pltpu.make_async_copy(vis.at[z], vis_hbm.at[z], sems.at[1 + z]).start()
+    weights.wait()
+    for z in range(2):
+        pltpu.make_async_copy(vis.at[z], vis_hbm.at[z], sems.at[1 + z]).wait()
 
 
 def per_device(chans, voltages, weights, sat_index, offsets, angles):
@@ -375,10 +398,10 @@
     vmem = pl.BlockSpec(memory_space=pltpu.VMEM)
     hbm = pl.BlockSpec(memory_space=pltpu.HBM)
     dma = pltpu.SemaphoreType.DMA
-    vis, new = pl.pallas_call(
+    wide, new = pl.pallas_call(
         functools.partial(kernel, chans),
         out_shape=(
-            jax.ShapeDtypeStruct((2, DISH, CH, ALL * ALL), F32),
+            jax.ShapeDtypeStruct((2 * CYC, ALLP * PER, TIME), F32),
             jax.ShapeDtypeStruct((2, DISH, BEAM, CH, PORT), BF16),
         ),
         in_specs=[hbm] * 5,
@@ -389,36 +412,50 @@
             pltpu.VMEM((CYC, 2), jnp.int32),
             pltpu.VMEM((CYC, TIME), jnp.int32),
             pltpu.VMEM((64, PORT), F32),
-            pltpu.VMEM((2, PER, ALL * ALL), F32),
             pltpu.VMEM((DISH, 2 * WR, LANES), BF16),
             pltpu.VMEM((CYC, 2), jnp.int32),
             pltpu.VMEM((CYC, 2), jnp.int32),
             pltpu.VMEM((CYC, 2, 8, LANES), F32),
             pltpu.VMEM((CYC, TILES, DISH * 8, TIME), F32),
-            pltpu.VMEM((CYC, 2, 2, 16, LANES), F32),
-            pltpu.VMEM((CYC, 2, 16, LANES), F32),
-            pltpu.VMEM((CYC, 2, 16, LANES), F32),
+            pltpu.VMEM((2, 24, LANES), F32),
+            pltpu.VMEM((CYC, 2, 24, LANES), F32),
+            pltpu.VMEM((CYC, 24, LANES), F32),
+            pltpu.VMEM((CYC, 24, LANES), F32),
             pltpu.VMEM((CYC, 32, LANES), F32),
             pltpu.VMEM((TILES, 64, TIME), F32),
             pltpu.VMEM((64, LANES), F32),
-            pltpu.VMEM((SEC, BLKP, 2 * TIME), F32),
-            pltpu.VMEM((CYC, SEC, BLKP, 2 * TIME), BF16),
-            pltpu.VMEM((CYC, SEC, BLKP, 2 * TIME), BF16),
-            pltpu.VMEM((2 * CYC, ALLP * PER, TIME), F32),
-            pltpu.VMEM((2, PER * ALLP, TIME), F32),
+            pltpu.VMEM((SEC, PARTS, BLKP, 2 * TIME), F32),
+            pltpu.VMEM((CYC, SEC, PARTS, BLKP, 2 * TIME), BF16),
+            pltpu.VMEM((CYC, SEC, PARTS, BLKP, 2 * TIME), BF16),
             dma((4,)),
             dma((CYC, DISH, 2)),
             dma((2,)),
             dma((2,)),
             dma((CYC, 2)),
             dma((CYC, 2)),
-            dma((CYC, SEC - 1)),
-            dma((CYC, SEC - 1)),
+            dma((CYC, PARTS, SEC - 1)),
+            dma((CYC, PARTS, SEC - 1)),
         ],
         compiler_params=pltpu.CompilerParams(
             collective_id=0, has_side_effects=True, vmem_limit_bytes=24 << 20
         ),
     )(*(pltpu.with_memory_space_constraint(a, pltpu.HBM) for a in (volt, w_in, sat, offsets, angles)))
+    vis, new = pl.pallas_call(
+        correlate,
+        out_shape=(
+            jax.ShapeDtypeStruct((2, DISH, CH, ALL * ALL), F32),
+            jax.ShapeDtypeStruct((2, DISH, BEAM, CH, PORT), BF16),
+        ),
+        in_specs=[vmem, vmem],
+        out_specs=(hbm, hbm),
+        scratch_shapes=[
+            pltpu.VMEM((2, DISH, CH, ALL * ALL), F32),
+            pltpu.VMEM((2, PER, ALL * ALL), F32),
+            pltpu.VMEM((2, PER * ALLP, TIME), F32),
+            dma((3,)),
+        ],
+        compiler_params=pltpu.CompilerParams(vmem_limit_bytes=24 << 20),
+    )(wide, new)
     return vis, new.transpose(0, 1, 3, 2, 4)
 
 

time: 30.6 us -> 29.4 us (0.961)
  local copies, waits for them, and re-layouts: 1.52 us -> 0 us
  Pallas kernels: 28.3 us -> 28.7 us
    pallas_call x0 -> x1, Pallas kernels: none -> 1.53 us  [per_device(): pl.pallas_call(correlate, out_shape=(jax.ShapeDtypeStruct((2, DISH, CH, A...]
    unnamed x2 -> x0, local copies, waits for them, and re-layouts: 1.52 us -> none
    pallas_call x1, Pallas kernels: 28.3 us -> 27.1 us  [per_device(): pl.pallas_call(functools.partial(kernel, chans), out_shape=(jax.ShapeDtyp...]
where the time goes in v2:
time: 29.4 us; the launch traced here: 29.3 us
  Pallas kernels  28.7 us (98%)
  between operations  0.64 us (2%)
    pallas_call x1, Pallas kernels, per_device(): pl.pallas_call(functools.partial(kernel, chans), out_shape=(jax.ShapeDtyp...  27.1 us
    pallas_call x1, Pallas kernels, per_device(): pl.pallas_call(correlate, out_shape=(jax.ShapeDtypeStruct((2, DISH, CH, A...  1.53 us

profile of v2, /device:TPU:257, one launch (start us, length us, event | category | flops | bytes accessed | tf_op | source)
XLA Modules:
  0.0 29.3 jit_solution(18011190207699577591)
XLA Ops:
  0.6 27.1 %shard_map.68 = (f32[4,720,128]{2,1,0:T(8,128)S(1)}, bf16[2,9,36,2,188]{4,3,2,1,0:T(2,128)(2,1)S(1)}) custom-call(bf16[2,2,9,376,128]{4,3,2,1,0:T(8,128)(2,1)} %bitcast.6, bf16[2,9,36,2,188]{4,3,2,1,0:T(2,128)(2,1)} %bitcast.7, s32[2,2]{1,0:T(2,128)} %bitcast.8, s32[2,128]{1,0:T(2,128)} %offs_hbm.1, f32[64,188]{1,0:T(8,128)} %ang_hbm.1), custom_call_target="tpu_custom_call" | custom-call | tf_op jit(solution)/shard_map/pallas_call | solution.py:401
  27.8 1.5 %shard_map.69 = (f32[2,9,2,1296]{3,2,1,0:T(2,128)}, bf16[2,9,36,2,188]{4,3,2,1,0:T(2,128)(2,1)}) custom-call(f32[4,720,128]{2,1,0:T(8,128)S(1)} %get-tuple-element.6.wide, bf16[2,9,36,2,188]{4,3,2,1,0:T(2,128)(2,1)S(1)} %get-tuple-element.7.w_new), custom_call_target="tpu_custom_call" | custom-call | tf_op jit(solution)/shard_map/pallas_call | solution.py:443

commit v3 on v2

--- a/solution.py
+++ b/solution.py
@@ -74,9 +74,17 @@
     def load(c, d, z):
         return pltpu.make_async_copy(
             volt.at[c, z, d],
-            x.at[c, d, pl.ds(0, ROWS), pl.ds(z * TIME, TIME)],
+            x.at[c, z, d, pl.ds(0, ROWS)],
             x_sem.at[c, d, z],
         )
+
+    def wait_voltages(c):
+        for d in range(DISH):
+            for z in range(2):
+                load(c, d, z).wait()
+
+    def voltage(c, d):
+        return jnp.concatenate([x[c, 0, d], x[c, 1, d]], axis=1)
 
     sat_l[...] = jnp.zeros_like(sat_l)
     sat_r[...] = jnp.zeros_like(sat_r)
@@ -132,7 +140,8 @@
     own = (iota((WR, LANES), 0) & 1) == (iota((WR, LANES), 1) & 1)
     for c in range(CYC):
         for d in range(DISH):
-            x[c, d, pl.ds(ROWS, LANES - ROWS), :] = jnp.zeros((LANES - ROWS, 2 * TIME), BF16)
+            for z in range(2):
+                x[c, z, d, pl.ds(ROWS, LANES - ROWS), :] = jnp.zeros((LANES - ROWS, TIME), BF16)
     wide[:, pl.ds(ALL * PER, (ALLP - ALL) * PER), :] = jnp.zeros(
         (2 * CYC, (ALLP - ALL) * PER, TIME), F32
     )
@@ -152,10 +161,7 @@
         if c == 1:
             project(dishes)
         for j, d in enumerate(dishes):
-            if c == 0:
-                load(c, d, 0).wait()
-                load(c, d, 1).wait()
-            both = dot(we[d], x[c, d])
+            both = dot(we[d], voltage(c, d))
             real = both[:WR, :TIME] + both[WR:, TIME:]
             imag = both[:WR, TIME:] - both[WR:, :TIME]
             for s in range(SEC):
@@ -181,6 +187,7 @@
             beam_copy(c, k, j).start()
         recv[c, sec, k] = sbuf[c, sec, k]
 
+    wait_voltages(0)
     for k in range(PARTS):
         beams(0, k)
         send_beams(0, k)
@@ -215,29 +222,32 @@
         times = (offs[pl.ds(c, 1), :] == iota((TIME, TIME), 0)).astype(F32).astype(BF16)
         count = dot_t(jnp.ones((8, TIME), BF16), times)
         probe = ana[c].astype(BF16)
-        for d in range(DISH):
-            if c == 1:
-                load(c, d, 0).wait()
-                load(c, d, 1).wait()
-            block = x[c, d]
-            out = dot(probe, block)
-            out = out[:16] + out[16:]
-            y_real = (out[:8, :TIME] + out[8:, TIME:]) * count
-            y_imag = (out[8:, :TIME] - out[:8, TIME:]) * count
-            lines = jnp.concatenate(
-                [
-                    jnp.concatenate([y_real, -y_imag], axis=1),
-                    jnp.concatenate([y_imag, y_real], axis=1),
-                ],
-                axis=0,
-            )
-            high, low = split(lines)
-            back = dot_t(jnp.concatenate([high, low], axis=0), block)
-            back = back[:16] + back[16:]
-            for i in range(2):
-                kept = jnp.where(even4, back[8 * i : 8 * i + 4], back[8 * i + 4 : 8 * i + 8])
-                for k in range(TILES):
-                    vv[c, k, pl.ds(8 * d + 4 * i, 4), :] = kept[:, k * TIME : (k + 1) * TIME]
+        for first in range(0, DISH, 9):
+            dishes = range(first, first + 9)
+            outs = [dot(probe, voltage(c, d)) for d in dishes]
+            lines = []
+            for out in outs:
+                out = out[:16] + out[16:]
+                y_real = (out[:8, :TIME] + out[8:, TIME:]) * count
+                y_imag = (out[8:, :TIME] - out[:8, TIME:]) * count
+                pair = jnp.concatenate(
+                    [
+                        jnp.concatenate([y_real, -y_imag], axis=1),
+                        jnp.concatenate([y_imag, y_real], axis=1),
+                    ],
+                    axis=0,
+                )
+                lines.append(jnp.concatenate(split(pair), axis=0))
+            backs = []
+            for j, d in enumerate(dishes):
+                block = voltage(c, d)
+                backs.append(dot_t(lines[j], block))
+            for d, back in zip(dishes, backs):
+                back = back[:16] + back[16:]
+                for i in range(2):
+                    kept = jnp.where(even4, back[8 * i : 8 * i + 4], back[8 * i + 4 : 8 * i + 8])
+                    for k in range(TILES):
+                        vv[c, k, pl.ds(8 * d + 4 * i, 4), :] = kept[:, k * TIME : (k + 1) * TIME]
 
     even = even_lanes((DISH, LANES))
 
@@ -270,6 +280,7 @@
     pack[...] = jnp.zeros_like(pack)
     null_vectors(0)
     send_halo(0)
+    wait_voltages(1)
     null_vectors(1)
     send_halo(1)
 
@@ -308,27 +319,36 @@
         for q, (t, v) in enumerate(((t0r, u0r), (t0i, u0i), (t1r, u1r), (t1i, u1i))):
             for k in range(TILES):
                 syn[k, pl.ds(16 * q, DISH), :] = t[:, k * TIME : (k + 1) * TIME]
-            nul[pl.ds(16 * q, DISH), :] = v
+                nul[k, pl.ds(16 * q, DISH), :] = v[:, k * TIME : (k + 1) * TIME]
 
     def project(dishes):
-        inner = []
+        inner, bases, changes = [], [], []
         for d in dishes:
-            high, low = split(strided(syn, pl.ds(d, 4, stride=16)))
-            old = we[d]
-            inner.append(dot_t(old, high) + dot_t(old, low))
-        for d, g in zip(dishes, inner):
-            gr, gi = g[:WR], g[WR:]
-            v = [nul[pl.ds(16 * q + d, 1), :] for q in range(4)]
-            new_r = we[d, pl.ds(0, WR), :].astype(F32)
-            new_i = we[d, pl.ds(WR, WR), :].astype(F32)
+            probe = jnp.concatenate(split(strided(syn, pl.ds(d, 4, stride=16))), axis=0)
+            inner.append([dot_t(probe, we[d, pl.ds(z * WR, WR), :]) for z in range(2)])
+        for d in dishes:
+            high, low = split(strided(nul, pl.ds(d, 4, stride=16)))
+            bases.append(jnp.concatenate([high, low, high], axis=0))
+        for outs, basis in zip(inner, bases):
+            gr, gi = (out[:4] + out[4:] for out in outs)
+            first, second = [], []
             for s in range(2):
-                cr = gr[:, 2 * s : 2 * s + 1] + gi[:, 2 * s + 1 : 2 * s + 2]
-                ci = gi[:, 2 * s : 2 * s + 1] - gr[:, 2 * s + 1 : 2 * s + 2]
-                vr, vi = v[2 * s], v[2 * s + 1]
-                new_r = new_r - (vr * cr - vi * ci)
-                new_i = new_i - (vr * ci + vi * cr)
-            we[d, pl.ds(0, WR), :] = jnp.where(own, new_r, 0.0).astype(BF16)
-            we[d, pl.ds(WR, WR), :] = jnp.where(own, new_i, 0.0).astype(BF16)
+                cr = gr[2 * s : 2 * s + 1] + gi[2 * s + 1 : 2 * s + 2]
+                ci = gi[2 * s : 2 * s + 1] - gr[2 * s + 1 : 2 * s + 2]
+                first += [cr, -ci]
+                second += [ci, cr]
+            for rows in (first, second):
+                c_high, c_low = split(jnp.concatenate(rows, axis=0))
+                amount = jnp.concatenate([c_high, c_high, c_low], axis=0)
+                changes.append(
+                    lax.dot_general(
+                        amount, basis, (((0,), (0,)), ((), ())), preferred_element_type=F32
+                    )
+                )
+        for d in dishes:
+            for z in range(2):
+                new = we[d, pl.ds(z * WR, WR), :].astype(F32) - changes.pop(0)
+                we[d, pl.ds(z * WR, WR), :] = jnp.where(own, new, 0.0).astype(BF16)
 
     project_vectors(0)
     for k in range(PARTS):
@@ -407,7 +427,7 @@
         in_specs=[hbm] * 5,
         out_specs=(vmem, vmem),
         scratch_shapes=[
-            pltpu.VMEM((CYC, DISH, LANES, 2 * TIME), BF16),
+            pltpu.VMEM((CYC, 2, DISH, LANES, TIME), BF16),
             pltpu.VMEM((2, DISH, BEAM, CH, PORT), BF16),
             pltpu.VMEM((CYC, 2), jnp.int32),
             pltpu.VMEM((CYC, TIME), jnp.int32),
@@ -423,7 +443,7 @@
             pltpu.VMEM((CYC, 24, LANES), F32),
             pltpu.VMEM((CYC, 32, LANES), F32),
             pltpu.VMEM((TILES, 64, TIME), F32),
-            pltpu.VMEM((64, LANES), F32),
+            pltpu.VMEM((TILES, 64, TIME), F32),
             pltpu.VMEM((SEC, PARTS, BLKP, 2 * TIME), F32),
             pltpu.VMEM((CYC, SEC, PARTS, BLKP, 2 * TIME), BF16),
             pltpu.VMEM((CYC, SEC, PARTS, BLKP, 2 * TIME), BF16),

time: 29.4 us -> 27.9 us (0.949)
  Pallas kernels: 28.7 us -> 27.2 us
    pallas_call x1, Pallas kernels: 27.1 us -> 25.6 us  [per_device(): pl.pallas_call(functools.partial(kernel, chans), out_shape=(jax.ShapeDtyp...]
where the time goes in v3:
time: 27.9 us; the launch traced here: 27.8 us
  Pallas kernels  27.2 us (97%)
  between operations  0.64 us (2%)
    pallas_call x1, Pallas kernels, per_device(): pl.pallas_call(functools.partial(kernel, chans), out_shape=(jax.ShapeDtyp...  25.6 us
    pallas_call x1, Pallas kernels, per_device(): pl.pallas_call(correlate, out_shape=(jax.ShapeDtypeStruct((2, DISH, CH, A...  1.53 us

profile of v3, /device:TPU:257, one launch (start us, length us, event | category | flops | bytes accessed | tf_op | source)
XLA Modules:
  0.0 27.8 jit_solution(16207128114620724741)
XLA Ops:
  0.6 25.6 %shard_map.68 = (f32[4,720,128]{2,1,0:T(8,128)S(1)}, bf16[2,9,36,2,188]{4,3,2,1,0:T(2,128)(2,1)S(1)}) custom-call(bf16[2,2,9,376,128]{4,3,2,1,0:T(8,128)(2,1)} %bitcast.6, bf16[2,9,36,2,188]{4,3,2,1,0:T(2,128)(2,1)} %bitcast.7, s32[2,2]{1,0:T(2,128)} %bitcast.8, s32[2,128]{1,0:T(2,128)} %offs_hbm.1, f32[64,188]{1,0:T(8,128)} %ang_hbm.1), custom_call_target="tpu_custom_call" | custom-call | tf_op jit(solution)/shard_map/pallas_call | solution.py:421
  26.3 1.5 %shard_map.69 = (f32[2,9,2,1296]{3,2,1,0:T(2,128)}, bf16[2,9,36,2,188]{4,3,2,1,0:T(2,128)(2,1)}) custom-call(f32[4,720,128]{2,1,0:T(8,128)S(1)} %get-tuple-element.6.wide, bf16[2,9,36,2,188]{4,3,2,1,0:T(2,128)(2,1)S(1)} %get-tuple-element.7.w_new), custom_call_target="tpu_custom_call" | custom-call | tf_op jit(solution)/shard_map/pallas_call | solution.py:463

commit v4 on v3

--- a/solution.py
+++ b/solution.py
@@ -190,7 +190,6 @@
     wait_voltages(0)
     for k in range(PARTS):
         beams(0, k)
-        send_beams(0, k)
 
     for side in range(2):
 
@@ -283,6 +282,8 @@
     wait_voltages(1)
     null_vectors(1)
     send_halo(1)
+    for k in range(PARTS):
+        send_beams(0, k)
 
     def lane_sum(v):
         e = jnp.sum(jnp.where(even, v, 0.0), axis=1, keepdims=True)

time: 27.9 us -> 28 us (level)
  no operation moved by 1% of the time
where the time goes in v4:
time: 28 us; the launch traced here: 27.8 us
  Pallas kernels  27.2 us (97%)
  between operations  0.64 us (2%)
    pallas_call x1, Pallas kernels, per_device(): pl.pallas_call(functools.partial(kernel, chans), out_shape=(jax.ShapeDtyp...  25.7 us
    pallas_call x1, Pallas kernels, per_device(): pl.pallas_call(correlate, out_shape=(jax.ShapeDtypeStruct((2, DISH, CH, A...  1.53 us

profile of v4, /device:TPU:257, one launch (start us, length us, event | category | flops | bytes accessed | tf_op | source)
XLA Modules:
  0.0 27.8 jit_solution(9724931471797400301)
XLA Ops:
  0.6 25.7 %shard_map.68 = (f32[4,720,128]{2,1,0:T(8,128)S(1)}, bf16[2,9,36,2,188]{4,3,2,1,0:T(2,128)(2,1)S(1)}) custom-call(bf16[2,2,9,376,128]{4,3,2,1,0:T(8,128)(2,1)} %bitcast.6, bf16[2,9,36,2,188]{4,3,2,1,0:T(2,128)(2,1)} %bitcast.7, s32[2,2]{1,0:T(2,128)} %bitcast.8, s32[2,128]{1,0:T(2,128)} %offs_hbm.1, f32[64,188]{1,0:T(8,128)} %ang_hbm.1), custom_call_target="tpu_custom_call" | custom-call | tf_op jit(solution)/shard_map/pallas_call | solution.py:422
  26.3 1.5 %shard_map.69 = (f32[2,9,2,1296]{3,2,1,0:T(2,128)}, bf16[2,9,36,2,188]{4,3,2,1,0:T(2,128)(2,1)}) custom-call(f32[4,720,128]{2,1,0:T(8,128)S(1)} %get-tuple-element.6.wide, bf16[2,9,36,2,188]{4,3,2,1,0:T(2,128)(2,1)S(1)} %get-tuple-element.7.w_new), custom_call_target="tpu_custom_call" | custom-call | tf_op jit(solution)/shard_map/pallas_call | solution.py:464

commit v5 on v3

--- a/solution.py
+++ b/solution.py
@@ -362,9 +362,10 @@
     for k in range(PARTS):
         project(range(PART * k, PART * (k + 1)))
     for d in range(DISH):
+        dense = dot(we[d], gather)
         for z in range(2):
-            dense = dot(we[d, pl.ds(z * WR, WR), :], gather).astype(BF16)
-            w_out[z, d] = dense.reshape(BEAM, CH, PORT)
+            part = dense[z * WR : (z + 1) * WR].astype(BF16)
+            w_out[z, d] = part.reshape(BEAM, CH, PORT)
 
     for c in range(CYC):
         for k in range(PARTS):

time: 27.9 us -> 27.9 us (level)
  no operation moved by 1% of the time
where the time goes in v5:
time: 27.9 us; the launch traced here: 27.8 us
  Pallas kernels  27.2 us (97%)
  between operations  0.64 us (2%)
    pallas_call x1, Pallas kernels, per_device(): pl.pallas_call(functools.partial(kernel, chans), out_shape=(jax.ShapeDtyp...  25.6 us
    pallas_call x1, Pallas kernels, per_device(): pl.pallas_call(correlate, out_shape=(jax.ShapeDtypeStruct((2, DISH, CH, A...  1.53 us

profile of v5, /device:TPU:257, one launch (start us, length us, event | category | flops | bytes accessed | tf_op | source)
XLA Modules:
  0.0 27.8 jit_solution(7950128320861547091)
XLA Ops:
  0.6 25.6 %shard_map.68 = (f32[4,720,128]{2,1,0:T(8,128)S(1)}, bf16[2,9,36,2,188]{4,3,2,1,0:T(2,128)(2,1)S(1)}) custom-call(bf16[2,2,9,376,128]{4,3,2,1,0:T(8,128)(2,1)} %bitcast.6, bf16[2,9,36,2,188]{4,3,2,1,0:T(2,128)(2,1)} %bitcast.7, s32[2,2]{1,0:T(2,128)} %bitcast.8, s32[2,128]{1,0:T(2,128)} %offs_hbm.1, f32[64,188]{1,0:T(8,128)} %ang_hbm.1), custom_call_target="tpu_custom_call" | custom-call | tf_op jit(solution)/shard_map/pallas_call | solution.py:422
  26.3 1.5 %shard_map.69 = (f32[2,9,2,1296]{3,2,1,0:T(2,128)}, bf16[2,9,36,2,188]{4,3,2,1,0:T(2,128)(2,1)}) custom-call(f32[4,720,128]{2,1,0:T(8,128)S(1)} %get-tuple-element.6.wide, bf16[2,9,36,2,188]{4,3,2,1,0:T(2,128)(2,1)S(1)} %get-tuple-element.7.w_new), custom_call_target="tpu_custom_call" | custom-call | tf_op jit(solution)/shard_map/pallas_call | solution.py:464
